TPU v7x, 32 devices: a whole 2x2x4 slice. The times are simulated.
32 devices in a mesh: dp: 8 (over z, x), rep: 4 (over y, core).
Axes of the slice: x: 2, y: 2, z: 4, core: 2. Of those that a mesh axis runs over, the one named last changes fastest.
Arguments:
- tokens: bfloat16 [8192, 2048], P(('rep', 'dp')), parts along dimension 0, may hold values from -12 to 12
- router: bfloat16 [8192, 8], P('rep'), parts along dimension 0, may hold values from -12 to 12
- w_gate: bfloat16 [8, 2048, 768], P('dp'), may hold values from -0.125 to 0.125
- w_up: bfloat16 [8, 2048, 768], P('dp'), may hold values from -0.125 to 0.125
- w_down: bfloat16 [8, 768, 2048], P('dp'), may hold values from -0.21875 to 0.21875
- picks: int32 [32, 32], P(('rep', 'dp')), parts along dimension 0, may hold values from 0 to 2047, as said below
Outputs:
- combined: bfloat16 [8192, 2048], P(('rep', 'dp')), parts along dimension 0
There are 4 independent parts, one for each index of `rep`. A program takes and returns all parts, laid end to end along the dimension named above; an argument that names none is the same for every part. Nothing has to cross between parts.
Inputs may be any that keep to these rules, and one draw needn't show every extreme that they name: `picks`: row e holds 32 different tokens taken by expert e, sorted by the device that holds them (256 tokens each, in order); at most 6 of them lie among one device's tokens, and in every row exactly 6 lie among some device's tokens.
All inputs are finite; a program needn't handle non-finite values.
Results may differ from a plain program's by a relative error of at most 0.0062.
Values may be sent and summed in bfloat16 or wider, within the bound.
No kernel may reach another device: no remote copies, remote signals or barrier semaphores. Data moves between devices by JAX's collectives and lax.ppermute only.
A program may use at most 64 MiB of HBM per device.

v0:
```python
import jax
import jax.numpy as jnp
from jax import lax
from jax.sharding import PartitionSpec as P

MOST = 6


def feed_forward(buffer_rows, gate_values, gate_w, up_w, down_w):
    gate_act = jnp.dot(buffer_rows, gate_w, preferred_element_type=jnp.float32)
    up_act = jnp.dot(buffer_rows, up_w, preferred_element_type=jnp.float32)
    hidden = (gate_values.astype(jnp.float32)[:, None] * jax.nn.silu(gate_act) * up_act).astype(
        jnp.bfloat16
    )
    return jnp.dot(hidden, down_w, preferred_element_type=jnp.float32).astype(jnp.bfloat16)


def body(tokens, router, w_gate, w_up, w_down, picks):
    sources = lax.axis_size("dp")
    tok_dev = tokens.shape[0]
    width = tokens.shape[1]
    experts = router.shape[1]
    my_picks = picks[0]
    capacity = my_picks.shape[0]
    logits = jnp.dot(tokens, router, preferred_element_type=jnp.float32)
    shares = jax.nn.softmax(logits, axis=1)
    source_of = my_picks // tok_dev
    block_ids = jnp.arange(sources, dtype=jnp.int32)
    counts = jnp.sum((source_of[None, :] == block_ids[:, None]).astype(jnp.int32), axis=1)
    starts = jnp.cumsum(counts) - counts
    slot_pos = jnp.arange(MOST, dtype=jnp.int32)
    within = jnp.arange(capacity, dtype=jnp.int32) - starts[source_of]
    flat_index = source_of * MOST + within
    position = jnp.clip(starts[:, None] + slot_pos[None, :], 0, capacity - 1)
    to_owner = jnp.where(
        slot_pos[None, :] < counts[:, None], my_picks[position] - block_ids[:, None] * tok_dev, -1
    )
    local_index = lax.all_to_all(to_owner, "dp", split_axis=0, concat_axis=0, tiled=True)
    live_slot = local_index >= 0
    safe_index = jnp.maximum(local_index, 0)
    send_rows = jnp.where(live_slot[:, :, None], tokens[safe_index], jnp.zeros((), tokens.dtype))
    columns = lax.all_to_all(
        shares.T.astype(jnp.bfloat16), "dp", split_axis=0, concat_axis=1, tiled=True
    ).astype(jnp.float32)
    gate_dense = (experts * columns[0][my_picks]).astype(jnp.bfloat16)
    received = lax.all_to_all(send_rows, "dp", split_axis=0, concat_axis=0, tiled=True)
    gate_flat = jnp.zeros((sources * MOST,), jnp.bfloat16).at[flat_index].set(gate_dense)
    buffer_rows = received.reshape(sources * MOST, width)
    expert_out = feed_forward(buffer_rows, gate_flat, w_gate[0], w_up[0], w_down[0])
    returned = lax.all_to_all(
        expert_out.reshape(sources, MOST, width), "dp", split_axis=0, concat_axis=0, tiled=True
    )
    onehot = (local_index.reshape(1, -1) == jnp.arange(tok_dev, dtype=jnp.int32)[:, None]).astype(
        jnp.bfloat16
    )
    combined = jnp.dot(
        onehot, returned.reshape(sources * MOST, width), preferred_element_type=jnp.float32
    )
    return combined.astype(jnp.bfloat16)


def solution(mesh):
    return jax.shard_map(
        body,
        mesh=mesh,
        in_specs=(
            P(("rep", "dp"), None),
            P("rep", None),
            P("dp", None, None),
            P("dp", None, None),
            P("dp", None, None),
            P(("rep", "dp"), None),
        ),
        out_specs=P(("rep", "dp"), None),
        check_vma=False,
    )
```

profile of v0, /device:TPU:0, one launch (start us, length us, event | category | flops | bytes accessed | tf_op | source)
XLA Modules:
  0.0 63.1 jit_solution(9098866142192156870)
XLA Ops:
  0.0 0.8 %fusion.32 = s32[32]{0:T(128)S(1)} fusion(s32[1,32]{1,0:T(1,128)} %param.11), kind=kLoop, calls=%fused_computation.61 | loop fusion | flops 480 | bytes 256 | tf_op jit(solution)/shard_map/eq | solution.py:29
  1.3 1.4 %gather_fusion = s32[48]{0:T(128)S(1)} fusion(s32[32]{0:T(128)} %bitcast.65, s32[1024]{0:T(1024)S(1)} %pad_clamp_fusion.3), kind=kCustom, calls=%fused_computation | custom fusion | bytes 576 | tf_op jit(solution)/shard_map/gather | solution.py:36
  3.5 7.3 %all-to-all-start = ((s32[8,1,6]{2,1,0:T(1,128)}), s32[8,1,6]{2,1,0:T(1,128)S(1)}, u32[]{:S(2)}, u32[]{:S(2)}) async-start(s32[8,1,6]{2,1,0:T(1,128)} %bitcast.4), calls=%async_computation | async-start | bytes 8192 | tf_op jit(solution)/shard_map/all_to_all | solution.py:38
  10.8 1.6 %fusion.36 = (f32[256]{0:T(256)S(1)}, f32[256,8]{0,1:T(8,128)S(1)}) fusion(bf16[256,2048]{1,0:T(8,128)(2,1)} %param.6, bf16[2048,8]{0,1:T(8,128)(2,1)S(1)} %copy-done.2), kind=kOutput, calls=%fused_computation.65 | convolution fusion | flops 8390400 | bytes 1090560 | tf_op jit(solution)/shard_map/dot_general | solution.py:25
  12.5 0.7 %gather_fusion.1 = s32[32]{0:T(128)S(1)} fusion(s32[8]{0:T(128)S(1)} %bitcast_subtract_fusion.1, s32[1024]{0:T(1024)S(1)} %get-tuple-element.11), kind=kCustom, calls=%fused_computation.1 | custom fusion | bytes 384 | tf_op jit(solution)/shard_map/gather | solution.py:32
  15.1 2.1 %all-to-all-done = s32[8,1,6]{2,1,0:T(1,128)S(1)} async-done(((s32[8,1,6]{2,1,0:T(1,128)}), s32[8,1,6]{2,1,0:T(1,128)S(1)}, u32[]{:S(2)}, u32[]{:S(2)}) %all-to-all-start) | async-done | bytes 224 | tf_op jit(solution)/shard_map/all_to_all | solution.py:38
  17.2 3.9 %all-to-all-start.1 = ((bf16[8,2,128]{2,1,0:T(2,128)(2,1)}), bf16[8,2,128]{2,1,0:T(2,128)(2,1)S(1)}, u32[]{:S(2)}, u32[]{:S(2)}) async-start(bf16[8,2,128]{2,1,0:T(2,128)(2,1)} %reshape.372), calls=%async_computation.1 | async-start | bytes 8192 | tf_op jit(solution)/shard_map/all_to_all | solution.py:42
  21.2 2.2 %gather_fusion.3 = bf16[48,2048]{1,0:T(8,128)(2,1)S(1)} fusion(bf16[256,2048]{1,0:T(8,128)(2,1)} %param.6, s32[1024]{0:T(1024)S(1)} %pad_clamp_fusion), kind=kCustom, calls=%fused_computation.3 | custom fusion | bytes 393408 | tf_op jit(solution)/shard_map/gather | solution.py:41
  23.5 0.8 %reshape.342 = bf16[8,6,2048]{2,1,0:T(8,128)(2,1)} reshape(bf16[48,2048]{1,0:T(8,128)(2,1)S(1)} %gather_fusion.3) | data formatting | bytes 393216 | tf_op jit(solution)/shard_map/gather | solution.py:41
  24.2 1.7 %broadcast_select_fusion = bf16[8,6,2048]{2,1,0:T(8,128)(2,1)} fusion(bf16[8,6,2048]{2,1,0:T(8,128)(2,1)} %reshape.342, pred[8,6]{1,0:T(8,128)(4,1)S(1)} %compare_bitcast_fusion), kind=kLoop, calls=%fused_computation.15 | loop fusion | flops 98304 | bytes 393264 | tf_op jit(solution)/shard_map/jit(_where)/select_n | solution.py:41
  26.0 1.6 %all-to-all-done.1 = bf16[8,2,128]{2,1,0:T(2,128)(2,1)S(1)} async-done(((bf16[8,2,128]{2,1,0:T(2,128)(2,1)}), bf16[8,2,128]{2,1,0:T(2,128)(2,1)S(1)}, u32[]{:S(2)}, u32[]{:S(2)}) %all-to-all-start.1) | async-done | bytes 4128 | tf_op jit(solution)/shard_map/all_to_all | solution.py:42
  27.6 4.4 %all-to-all-start.2 = ((bf16[8,6,2048]{2,1,0:T(8,128)(2,1)}), bf16[8,6,2048]{2,1,0:T(8,128)(2,1)}, u32[]{:S(2)}, u32[]{:S(2)}) async-start(bf16[8,6,2048]{2,1,0:T(8,128)(2,1)} %broadcast_select_fusion), calls=%async_computation.2 | async-start | bytes 524288 | tf_op jit(solution)/shard_map/all_to_all | solution.py:46
  32.0 0.7 %gather_fusion.2 = f32[32]{0:T(128)S(1)} fusion(f32[2048]{0:T(1024)S(1)} %bitcast.66, s32[1024]{0:T(1024)S(1)} %get-tuple-element.10), kind=kCustom, calls=%fused_computation.2 | custom fusion | bytes 384 | tf_op jit(solution)/shard_map/gather | solution.py:45
  32.7 0.8 %scatter_custom_fusion = bf16[48]{0:T(256)(128)(2,1)S(1)} fusion(s32[32]{0:T(128)S(1)} %fusion.30, bf16[32]{0:T(256)(128)(2,1)S(1)} %multiply_convert_fusion, bf16[]{:T(256)} %constant.14.clone.1), kind=kCustom, calls=%fused_computation.62 | custom fusion | bytes 98 | tf_op jit(solution)/shard_map/scatter | solution.py:47
  33.5 6.8 %all-to-all-done.2 = bf16[8,6,2048]{2,1,0:T(8,128)(2,1)} async-done(((bf16[8,6,2048]{2,1,0:T(8,128)(2,1)}), bf16[8,6,2048]{2,1,0:T(8,128)(2,1)}, u32[]{:S(2)}, u32[]{:S(2)}) %all-to-all-start.2) | async-done | bytes 196640 | tf_op jit(solution)/shard_map/all_to_all | solution.py:46
  40.3 1.0 %reshape.313 = bf16[48,2048]{1,0:T(8,128)(2,1)S(1)} reshape(bf16[8,6,2048]{2,1,0:T(8,128)(2,1)} %all-to-all-done.2) | data formatting | bytes 393216 | tf_op jit(solution)/shard_map/reshape | solution.py:48
  41.3 3.2 %fusion.4 = f32[48,768]{1,0:T(8,128)} fusion(bf16[48,2048]{1,0:T(8,128)(2,1)S(1)} %reshape.313, bf16[1,2048,768]{2,1,0:T(8,128)(2,1)} %param.8), kind=kOutput, calls=%fused_computation.9 | convolution fusion | flops 150994944 | bytes 3489792 | tf_op jit(solution)/shard_map/dot_general | solution.py:10
  44.5 3.2 %fusion.6 = bf16[48,2048]{1,0:T(8,128)(2,1)S(1)} fusion(bf16[1,768,2048]{2,1,0:T(8,128)(2,1)S(1)} %copy-done, bf16[48,2048]{1,0:T(8,128)(2,1)S(1)} %reshape.313, bf16[1,2048,768]{2,1,0:T(8,128)(2,1)} %param.9, f32[48,768]{1,0:T(8,128)} %fusion.4, f32[48]{0:T(128)S(1)} %convert_element_type.40), kind=kOutput, calls=%fused_computation.12 | convolution fusion | flops 302346240 | bytes 6832320 | tf_op jit(solution)/shard_map/dot_general | solution.py:15
  47.7 0.8 %reshape.314 = bf16[8,6,2048]{2,1,0:T(8,128)(2,1)} reshape(bf16[48,2048]{1,0:T(8,128)(2,1)S(1)} %fusion.6) | data formatting | bytes 393216 | tf_op jit(solution)/shard_map/reshape | solution.py:51
  48.5 3.4 %all-to-all-start.3 = ((bf16[8,6,2048]{2,1,0:T(8,128)(2,1)}), bf16[8,6,2048]{2,1,0:T(8,128)(2,1)S(1)}, u32[]{:S(2)}, u32[]{:S(2)}) async-start(bf16[8,6,2048]{2,1,0:T(8,128)(2,1)} %reshape.314), calls=%async_computation.3 | async-start | bytes 524288 | tf_op jit(solution)/shard_map/all_to_all | solution.py:50
  52.5 0.7 %reduce.3 = s32[8,6]{1,0:T(8,128)S(1)} reduce(s32[8,1,6]{2,1,0:T(1,128)S(1)} %all-to-all-done, s32[]{:T(128)} %broadcast.285), dimensions={1}, to_apply=%all_to_all.20.reduce_sub_computation.3 | reduce | bytes 388 | tf_op jit(solution)/shard_map/all_to_all | solution.py:38
  53.3 6.8 %all-to-all-done.3 = bf16[8,6,2048]{2,1,0:T(8,128)(2,1)S(1)} async-done(((bf16[8,6,2048]{2,1,0:T(8,128)(2,1)}), bf16[8,6,2048]{2,1,0:T(8,128)(2,1)S(1)}, u32[]{:S(2)}, u32[]{:S(2)}) %all-to-all-start.3) | async-done | bytes 196640 | tf_op jit(solution)/shard_map/all_to_all | solution.py:50
  60.1 0.7 %reshape.315 = bf16[48,2048]{1,0:T(8,128)(2,1)} reshape(bf16[8,6,2048]{2,1,0:T(8,128)(2,1)S(1)} %all-to-all-done.3) | data formatting | bytes 393216 | tf_op jit(solution)/shard_map/reshape | solution.py:57
  60.8 2.3 %convolution_convert_fusion = bf16[256,2048]{1,0:T(8,128)(2,1)} fusion(bf16[48,2048]{1,0:T(8,128)(2,1)} %reshape.315, s32[48]{0:T(128)S(1)} %eq.34), kind=kOutput, calls=%fused_computation.11 | convolution fusion | flops 50868224 | bytes 1245376 | tf_op jit(solution)/shard_map/dot_general | solution.py:56
  (33 shorter events, 4.0 us)
Async XLA Ops:
  0.0 44.5 %copy-start = (bf16[1,768,2048]{2,1,0:T(8,128)(2,1)S(1)}, bf16[1,768,2048]{2,1,0:T(8,128)(2,1)}, u32[]{:S(2)}) copy-start(bf16[1,768,2048]{2,1,0:T(8,128)(2,1)} %param.10) | copy-start | bytes 9437188
  0.0 10.8 %copy-start.1 = (s32[1,32]{1,0:T(1,128)S(1)}, s32[1,32]{1,0:T(1,128)}, u32[]{:S(2)}) copy-start(s32[1,32]{1,0:T(1,128)} %param.11) | copy-start | bytes 388
  0.0 10.8 %copy-start.2 = (bf16[2048,8]{0,1:T(8,128)(2,1)S(1)}, bf16[2048,8]{0,1:T(8,128)(2,1)}, u32[]{:S(2)}) copy-start(bf16[2048,8]{0,1:T(8,128)(2,1)} %param.7) | copy-start | bytes 98308
  3.5 13.7 %all-to-all-start = ((s32[8,1,6]{2,1,0:T(1,128)}), s32[8,1,6]{2,1,0:T(1,128)S(1)}, u32[]{:S(2)}, u32[]{:S(2)}) async-start(s32[8,1,6]{2,1,0:T(1,128)} %bitcast.4), calls=%async_computation | async-start | bytes 8192 | tf_op jit(solution)/shard_map/all_to_all | solution.py:38
  17.2 10.4 %all-to-all-start.1 = ((bf16[8,2,128]{2,1,0:T(2,128)(2,1)}), bf16[8,2,128]{2,1,0:T(2,128)(2,1)S(1)}, u32[]{:S(2)}, u32[]{:S(2)}) async-start(bf16[8,2,128]{2,1,0:T(2,128)(2,1)} %reshape.372), calls=%async_computation.1 | async-start | bytes 8192 | tf_op jit(solution)/shard_map/all_to_all | solution.py:42
  27.6 12.7 %all-to-all-start.2 = ((bf16[8,6,2048]{2,1,0:T(8,128)(2,1)}), bf16[8,6,2048]{2,1,0:T(8,128)(2,1)}, u32[]{:S(2)}, u32[]{:S(2)}) async-start(bf16[8,6,2048]{2,1,0:T(8,128)(2,1)} %broadcast_select_fusion), calls=%async_computation.2 | async-start | bytes 524288 | tf_op jit(solution)/shard_map/all_to_all | solution.py:46
  48.5 11.6 %all-to-all-start.3 = ((bf16[8,6,2048]{2,1,0:T(8,128)(2,1)}), bf16[8,6,2048]{2,1,0:T(8,128)(2,1)S(1)}, u32[]{:S(2)}, u32[]{:S(2)}) async-start(bf16[8,6,2048]{2,1,0:T(8,128)(2,1)} %reshape.314), calls=%async_computation.3 | async-start | bytes 524288 | tf_op jit(solution)/shard_map/all_to_all | solution.py:50
where the time goes:
time: 63.7 us; the launch traced here: 63.1 us
  starting transfers between devices  19 us (30%)
  waiting for transfers between devices  17.3 us (27%)
  local copies, waits for them, and re-layouts  11.3 us (18%)
  matrix products  10.3 us (16%)
  other arithmetic  5.13 us (8%)
    all_to_all x1, starting transfers between devices, body(): lax.all_to_all(to_owner, 'dp', split_axis=0, concat_axis=0, tiled=True)  7.29 us
    all_to_all x1, waiting for transfers between devices, body(): lax.all_to_all(send_rows, 'dp', split_axis=0, concat_axis=0, tiled=True)  6.8 us
    all_to_all x1, waiting for transfers between devices, body(): lax.all_to_all(expert_out.reshape(sources, MOST, width), 'dp', split_axis...  6.78 us
    all_to_all x1, starting transfers between devices, body(): lax.all_to_all(send_rows, 'dp', split_axis=0, concat_axis=0, tiled=True)  4.37 us
    all_to_all x1, starting transfers between devices, body(): lax.all_to_all(shares.T.astype(jnp.bfloat16), 'dp', split_axis=0, concat_...  3.9 us
    all_to_all x1, starting transfers between devices, body(): lax.all_to_all(expert_out.reshape(sources, MOST, width), 'dp', split_axis...  3.41 us
    dot_general x1, matrix products, feed_forward(): jnp.dot(hidden, down_w, preferred_element_type=jnp.float32)  3.19 us
    dot_general x1, matrix products, feed_forward(): gate_act = jnp.dot(buffer_rows, gate_w, preferred_element_type=jnp.float32)  3.18 us
  transfers between devices with their start and end apart: 4, of which 4 were waited for; matrix products, arithmetic and copies ran while one was open for 19% of the time, Pallas kernels for 0%

commit v1 on v0

--- a/solution.py
+++ b/solution.py
@@ -4,6 +4,18 @@
 from jax.sharding import PartitionSpec as P
 
 MOST = 6
+
+
+def exchange_directly(x, axis, split, join):
+    ways, here = (lax.axis_size(axis), lax.axis_index(axis))
+    width = x.shape[split] // ways
+    turned = jnp.roll(x, -here * width, axis=split)
+    got = [lax.slice_in_dim(turned, 0, width, axis=split)]
+    for far in range(1, ways):
+        sent = lax.slice_in_dim(turned, far * width, (far + 1) * width, axis=split)
+        got.append(lax.ppermute(sent, axis, [(d, (d + far) % ways) for d in range(ways)]))
+    line = jnp.concatenate(got[::-1], axis=join)
+    return jnp.roll(line, (here + 1) * got[0].shape[join], axis=join)
 
 
 def feed_forward(buffer_rows, gate_values, gate_w, up_w, down_w):
@@ -35,7 +47,7 @@
     to_owner = jnp.where(
         slot_pos[None, :] < counts[:, None], my_picks[position] - block_ids[:, None] * tok_dev, -1
     )
-    local_index = lax.all_to_all(to_owner, "dp", split_axis=0, concat_axis=0, tiled=True)
+    local_index = exchange_directly(to_owner, "dp", 0, 0)
     live_slot = local_index >= 0
     safe_index = jnp.maximum(local_index, 0)
     send_rows = jnp.where(live_slot[:, :, None], tokens[safe_index], jnp.zeros((), tokens.dtype))

time: 63.7 us -> 70.9 us (1.11)
  starting transfers between devices: 19 us -> 28.4 us
  other arithmetic: 5.13 us -> 3.81 us
    ppermute x0 -> x7, starting transfers between devices: none -> 16.3 us  [exchange_directly(): lax.ppermute(sent, axis, [(d, (d + far) % ways) for d in range(ways)])]
    all_to_all x1 -> x0, starting transfers between devices: 7.29 us -> none  [body(): lax.all_to_all(to_owner, 'dp', split_axis=0, concat_axis=0, tiled=True)]
    ppermute x0 -> x7, waiting for transfers between devices: none -> 2.11 us  [exchange_directly(): lax.ppermute(sent, axis, [(d, (d + far) % ways) for d in range(ways)])]
    all_to_all x1 -> x0, waiting for transfers between devices: 2.1 us -> none  [body(): lax.all_to_all(to_owner, 'dp', split_axis=0, concat_axis=0, tiled=True)]
    all_to_all x1, waiting for transfers between devices: 1.63 us -> 0.01 us  [body(): lax.all_to_all(shares.T.astype(jnp.bfloat16), 'dp', split_axis=0, concat_...]
    all_to_all x1, waiting for transfers between devices: 6.78 us -> 8.08 us  [body(): lax.all_to_all(expert_out.reshape(sources, MOST, width), 'dp', split_axis...]
    all_to_all x1, starting transfers between devices: 4.37 us -> 5.43 us  [body(): lax.all_to_all(send_rows, 'dp', split_axis=0, concat_axis=0, tiled=True)]
  transfers between devices with their start and end apart: 4 -> 10, of which waited for: 4 -> 3; matrix products, arithmetic and copies ran while one was open for 19% -> 15% of each run, Pallas kernels for 0% -> 0%
where the time goes in v1:
time: 70.9 us; the launch traced here: 70.3 us
  starting transfers between devices  28.4 us (40%)
  waiting for transfers between devices  17 us (24%)
  local copies, waits for them, and re-layouts  10.6 us (15%)
  matrix products  10.3 us (15%)
  other arithmetic  3.81 us (5%)
    ppermute x7, starting transfers between devices, exchange_directly(): lax.ppermute(sent, axis, [(d, (d + far) % ways) for d in range(ways)])  16.3 us
    all_to_all x1, waiting for transfers between devices, body(): lax.all_to_all(expert_out.reshape(sources, MOST, width), 'dp', split_axis...  8.08 us
    all_to_all x1, waiting for transfers between devices, body(): lax.all_to_all(send_rows, 'dp', split_axis=0, concat_axis=0, tiled=True)  6.8 us
    all_to_all x1, starting transfers between devices, body(): lax.all_to_all(send_rows, 'dp', split_axis=0, concat_axis=0, tiled=True)  5.43 us
    all_to_all x1, starting transfers between devices, body(): lax.all_to_all(expert_out.reshape(sources, MOST, width), 'dp', split_axis...  3.41 us
    all_to_all x1, starting transfers between devices, body(): lax.all_to_all(shares.T.astype(jnp.bfloat16), 'dp', split_axis=0, concat_...  3.26 us
    dot_general x1, matrix products, feed_forward(): jnp.dot(hidden, down_w, preferred_element_type=jnp.float32)  3.2 us
    dot_general x1, matrix products, feed_forward(): gate_act = jnp.dot(buffer_rows, gate_w, preferred_element_type=jnp.float32)  3.18 us
  transfers between devices with their start and end apart: 10, of which 3 were waited for; matrix products, arithmetic and copies ran while one was open for 15% of the time, Pallas kernels for 0%

profile of v1, /device:TPU:0, one launch (start us, length us, event | category | flops | bytes accessed | tf_op | source)
XLA Modules:
  0.0 70.3 jit_solution(13822636822109079678)
XLA Ops:
  0.0 0.8 %fusion.34 = s32[32]{0:T(128)S(1)} fusion(s32[1,32]{1,0:T(1,128)} %param.13), kind=kLoop, calls=%fused_computation.67 | loop fusion | flops 480 | bytes 256 | tf_op jit(solution)/shard_map/eq | solution.py:41
  1.3 1.4 %gather_fusion = s32[48]{0:T(128)S(1)} fusion(s32[32]{0:T(128)} %bitcast.58, s32[1024]{0:T(1024)S(1)} %pad_clamp_fusion.3), kind=kCustom, calls=%fused_computation | custom fusion | bytes 576 | tf_op jit(solution)/shard_map/gather | solution.py:48
  3.0 3.0 %collective-permute-start.6 = (s32[1,6]{1,0:T(1,128)S(1)}, s32[1,6]{1,0:T(1,128)S(1)}, u32[]{:S(2)}, u32[]{:S(2)}) collective-permute-start(s32[1,6]{1,0:T(1,128)S(1)} %get-tuple-element.11), channel_id=1, source_target_pairs={{0,4},{4,8},{8,12},{12,16},{16,20},{20,24},{24,28},{28,0},{1,5},{5... | collective-permute-start | bytes 80 | tf_op jit(solution)/shard_map/ppermute | solution.py:16
  6.0 1.6 %collective-permute-start.5 = (s32[1,6]{1,0:T(1,128)S(1)}, s32[1,6]{1,0:T(1,128)S(1)}, u32[]{:S(2)}, u32[]{:S(2)}) collective-permute-start(s32[1,6]{1,0:T(1,128)S(1)} %get-tuple-element.12), channel_id=1, source_target_pairs={{0,8},{4,12},{8,16},{12,20},{16,24},{20,28},{24,0},{28,4},{1,9},{5... | collective-permute-start | bytes 80 | tf_op jit(solution)/shard_map/ppermute | solution.py:16
  7.6 2.6 %collective-permute-start.4 = (s32[1,6]{1,0:T(1,128)S(1)}, s32[1,6]{1,0:T(1,128)S(1)}, u32[]{:S(2)}, u32[]{:S(2)}) collective-permute-start(s32[1,6]{1,0:T(1,128)S(1)} %get-tuple-element.13), channel_id=1, source_target_pairs={{0,12},{4,16},{8,20},{12,24},{16,28},{20,0},{24,4},{28,8},{1,13},{... | collective-permute-start | bytes 80 | tf_op jit(solution)/shard_map/ppermute | solution.py:16
  10.1 1.2 %collective-permute-start.3 = (s32[1,6]{1,0:T(1,128)S(1)}, s32[1,6]{1,0:T(1,128)S(1)}, u32[]{:S(2)}, u32[]{:S(2)}) collective-permute-start(s32[1,6]{1,0:T(1,128)S(1)} %get-tuple-element.14), channel_id=1, source_target_pairs={{0,16},{4,20},{8,24},{12,28},{16,0},{20,4},{24,8},{28,12},{1,17},{... | collective-permute-start | bytes 80 | tf_op jit(solution)/shard_map/ppermute | solution.py:16
  11.4 2.6 %collective-permute-start.2 = (s32[1,6]{1,0:T(1,128)S(1)}, s32[1,6]{1,0:T(1,128)S(1)}, u32[]{:S(2)}, u32[]{:S(2)}) collective-permute-start(s32[1,6]{1,0:T(1,128)S(1)} %get-tuple-element.15), channel_id=1, source_target_pairs={{0,20},{4,24},{8,28},{12,0},{16,4},{20,8},{24,12},{28,16},{1,21},{... | collective-permute-start | bytes 80 | tf_op jit(solution)/shard_map/ppermute | solution.py:16
  14.0 1.6 %fusion.40 = (f32[256]{0:T(256)S(1)}, f32[256,8]{0,1:T(8,128)S(1)}) fusion(bf16[256,2048]{1,0:T(8,128)(2,1)} %param.8, bf16[2048,8]{0,1:T(8,128)(2,1)S(1)} %copy-done.2), kind=kOutput, calls=%fused_computation.72 | convolution fusion | flops 8390400 | bytes 1090560 | tf_op jit(solution)/shard_map/dot_general | solution.py:37
  17.4 3.3 %all-to-all-start = ((bf16[8,2,128]{2,1,0:T(2,128)(2,1)}), bf16[8,2,128]{2,1,0:T(2,128)(2,1)S(1)}, u32[]{:S(2)}, u32[]{:S(2)}) async-start(bf16[8,2,128]{2,1,0:T(2,128)(2,1)} %reshape.287), calls=%async_computation | async-start | bytes 8192 | tf_op jit(solution)/shard_map/all_to_all | solution.py:54
  21.5 3.8 %collective-permute-start.1 = (s32[1,6]{1,0:T(1,128)S(1)}, s32[1,6]{1,0:T(1,128)S(1)}, u32[]{:S(2)}, u32[]{:S(2)}) collective-permute-start(s32[1,6]{1,0:T(1,128)S(1)} %get-tuple-element.16), channel_id=1, source_target_pairs={{0,24},{4,28},{8,0},{12,4},{16,8},{20,12},{24,16},{28,20},{1,25},{... | collective-permute-start | bytes 80 | tf_op jit(solution)/shard_map/ppermute | solution.py:16
  25.2 1.5 %collective-permute-start = (s32[1,6]{1,0:T(1,128)S(1)}, s32[1,6]{1,0:T(1,128)S(1)}, u32[]{:S(2)}, u32[]{:S(2)}) collective-permute-start(s32[1,6]{1,0:T(1,128)S(1)} %get-tuple-element.17), channel_id=1, source_target_pairs={{0,28},{4,0},{8,4},{12,8},{16,12},{20,16},{24,20},{28,24},{1,29},{... | collective-permute-start | bytes 80 | tf_op jit(solution)/shard_map/ppermute | solution.py:16
  26.7 2.1 %collective-permute-done = s32[1,6]{1,0:T(1,128)S(1)} collective-permute-done((s32[1,6]{1,0:T(1,128)S(1)}, s32[1,6]{1,0:T(1,128)S(1)}, u32[]{:S(2)}, u32[]{:S(2)}) %collective-permute-start) | collective-permute-done | bytes 56 | tf_op jit(solution)/shard_map/ppermute | solution.py:16
  29.0 2.2 %gather_fusion.3 = bf16[48,2048]{1,0:T(8,128)(2,1)S(1)} fusion(bf16[256,2048]{1,0:T(8,128)(2,1)} %param.8, s32[1024]{0:T(1024)S(1)} %pad_clamp_fusion), kind=kCustom, calls=%fused_computation.3 | custom fusion | bytes 393408 | tf_op jit(solution)/shard_map/gather | solution.py:53
  31.2 0.8 %reshape.267 = bf16[8,6,2048]{2,1,0:T(8,128)(2,1)} reshape(bf16[48,2048]{1,0:T(8,128)(2,1)S(1)} %gather_fusion.3) | data formatting | bytes 393216 | tf_op jit(solution)/shard_map/gather | solution.py:53
  32.0 1.7 %broadcast_select_fusion = bf16[8,6,2048]{2,1,0:T(8,128)(2,1)} fusion(bf16[8,6,2048]{2,1,0:T(8,128)(2,1)} %reshape.267, pred[8,6]{1,0:T(8,128)(4,1)S(1)} %get-tuple-element.8), kind=kLoop, calls=%fused_computation.15 | loop fusion | flops 98304 | bytes 393264 | tf_op jit(solution)/shard_map/jit(_where)/select_n | solution.py:53
  33.7 5.4 %all-to-all-start.1 = ((bf16[8,6,2048]{2,1,0:T(8,128)(2,1)}), bf16[8,6,2048]{2,1,0:T(8,128)(2,1)}, u32[]{:S(2)}, u32[]{:S(2)}) async-start(bf16[8,6,2048]{2,1,0:T(8,128)(2,1)} %broadcast_select_fusion), calls=%async_computation.1 | async-start | bytes 524288 | tf_op jit(solution)/shard_map/all_to_all | solution.py:58
  40.7 6.8 %all-to-all-done.1 = bf16[8,6,2048]{2,1,0:T(8,128)(2,1)} async-done(((bf16[8,6,2048]{2,1,0:T(8,128)(2,1)}), bf16[8,6,2048]{2,1,0:T(8,128)(2,1)}, u32[]{:S(2)}, u32[]{:S(2)}) %all-to-all-start.1) | async-done | bytes 196640 | tf_op jit(solution)/shard_map/all_to_all | solution.py:58
  47.5 1.0 %reshape.238 = bf16[48,2048]{1,0:T(8,128)(2,1)S(1)} reshape(bf16[8,6,2048]{2,1,0:T(8,128)(2,1)} %all-to-all-done.1) | data formatting | bytes 393216 | tf_op jit(solution)/shard_map/reshape | solution.py:60
  48.5 3.2 %fusion.4 = f32[48,768]{1,0:T(8,128)} fusion(bf16[48,2048]{1,0:T(8,128)(2,1)S(1)} %reshape.238, bf16[1,2048,768]{2,1,0:T(8,128)(2,1)} %param.10), kind=kOutput, calls=%fused_computation.9 | convolution fusion | flops 150994944 | bytes 3489792 | tf_op jit(solution)/shard_map/dot_general | solution.py:22
  51.7 3.2 %fusion.6 = bf16[48,2048]{1,0:T(8,128)(2,1)S(1)} fusion(bf16[1,768,2048]{2,1,0:T(8,128)(2,1)S(1)} %copy-done, bf16[48,2048]{1,0:T(8,128)(2,1)S(1)} %reshape.238, bf16[1,2048,768]{2,1,0:T(8,128)(2,1)} %param.11, f32[48,768]{1,0:T(8,128)} %fusion.4, f32[48]{0:T(128)S(1)} %convert_element_type.40), kind=kOutput, calls=%fused_computation.12 | convolution fusion | flops 302346240 | bytes 6832320 | tf_op jit(solution)/shard_map/dot_general | solution.py:27
  54.9 0.8 %reshape.239 = bf16[8,6,2048]{2,1,0:T(8,128)(2,1)} reshape(bf16[48,2048]{1,0:T(8,128)(2,1)S(1)} %fusion.6) | data formatting | bytes 393216 | tf_op jit(solution)/shard_map/reshape | solution.py:63
  55.7 3.4 %all-to-all-start.2 = ((bf16[8,6,2048]{2,1,0:T(8,128)(2,1)}), bf16[8,6,2048]{2,1,0:T(8,128)(2,1)S(1)}, u32[]{:S(2)}, u32[]{:S(2)}) async-start(bf16[8,6,2048]{2,1,0:T(8,128)(2,1)} %reshape.239), calls=%async_computation.2 | async-start | bytes 524288 | tf_op jit(solution)/shard_map/all_to_all | solution.py:62
  59.2 8.1 %all-to-all-done.2 = bf16[8,6,2048]{2,1,0:T(8,128)(2,1)S(1)} async-done(((bf16[8,6,2048]{2,1,0:T(8,128)(2,1)}), bf16[8,6,2048]{2,1,0:T(8,128)(2,1)S(1)}, u32[]{:S(2)}, u32[]{:S(2)}) %all-to-all-start.2) | async-done | bytes 196640 | tf_op jit(solution)/shard_map/all_to_all | solution.py:62
  68.0 2.3 %convolution_convert_fusion = bf16[256,2048]{1,0:T(8,128)(2,1)} fusion(bf16[48,2048]{1,0:T(8,128)(2,1)} %reshape.240, s32[48]{0:T(128)S(1)} %eq.36), kind=kOutput, calls=%fused_computation.11 | convolution fusion | flops 50868224 | bytes 1245376 | tf_op jit(solution)/shard_map/dot_general | solution.py:68
  (46 shorter events, 5.7 us)
Async XLA Ops:
  0.0 51.7 %copy-start = (bf16[1,768,2048]{2,1,0:T(8,128)(2,1)S(1)}, bf16[1,768,2048]{2,1,0:T(8,128)(2,1)}, u32[]{:S(2)}) copy-start(bf16[1,768,2048]{2,1,0:T(8,128)(2,1)} %param.12) | copy-start | bytes 9437188
  0.0 20.7 %copy-start.1 = (s32[1,32]{1,0:T(1,128)S(1)}, s32[1,32]{1,0:T(1,128)}, u32[]{:S(2)}) copy-start(s32[1,32]{1,0:T(1,128)} %param.13) | copy-start | bytes 388
  0.0 14.0 %copy-start.2 = (bf16[2048,8]{0,1:T(8,128)(2,1)S(1)}, bf16[2048,8]{0,1:T(8,128)(2,1)}, u32[]{:S(2)}) copy-start(bf16[2048,8]{0,1:T(8,128)(2,1)} %param.9) | copy-start | bytes 98308
  3.0 18.5 %collective-permute-start.6 = (s32[1,6]{1,0:T(1,128)S(1)}, s32[1,6]{1,0:T(1,128)S(1)}, u32[]{:S(2)}, u32[]{:S(2)}) collective-permute-start(s32[1,6]{1,0:T(1,128)S(1)} %get-tuple-element.11), channel_id=1, source_target_pairs={{0,4},{4,8},{8,12},{12,16},{16,20},{20,24},{24,28},{28,0},{1,5},{5... | collective-permute-start | bytes 80 | tf_op jit(solution)/shard_map/ppermute | solution.py:16
  6.0 19.3 %collective-permute-start.5 = (s32[1,6]{1,0:T(1,128)S(1)}, s32[1,6]{1,0:T(1,128)S(1)}, u32[]{:S(2)}, u32[]{:S(2)}) collective-permute-start(s32[1,6]{1,0:T(1,128)S(1)} %get-tuple-element.12), channel_id=1, source_target_pairs={{0,8},{4,12},{8,16},{12,20},{16,24},{20,28},{24,0},{28,4},{1,9},{5... | collective-permute-start | bytes 80 | tf_op jit(solution)/shard_map/ppermute | solution.py:16
  7.6 19.1 %collective-permute-start.4 = (s32[1,6]{1,0:T(1,128)S(1)}, s32[1,6]{1,0:T(1,128)S(1)}, u32[]{:S(2)}, u32[]{:S(2)}) collective-permute-start(s32[1,6]{1,0:T(1,128)S(1)} %get-tuple-element.13), channel_id=1, source_target_pairs={{0,12},{4,16},{8,20},{12,24},{16,28},{20,0},{24,4},{28,8},{1,13},{... | collective-permute-start | bytes 80 | tf_op jit(solution)/shard_map/ppermute | solution.py:16
  10.1 16.6 %collective-permute-start.3 = (s32[1,6]{1,0:T(1,128)S(1)}, s32[1,6]{1,0:T(1,128)S(1)}, u32[]{:S(2)}, u32[]{:S(2)}) collective-permute-start(s32[1,6]{1,0:T(1,128)S(1)} %get-tuple-element.14), channel_id=1, source_target_pairs={{0,16},{4,20},{8,24},{12,28},{16,0},{20,4},{24,8},{28,12},{1,17},{... | collective-permute-start | bytes 80 | tf_op jit(solution)/shard_map/ppermute | solution.py:16
  11.4 15.3 %collective-permute-start.2 = (s32[1,6]{1,0:T(1,128)S(1)}, s32[1,6]{1,0:T(1,128)S(1)}, u32[]{:S(2)}, u32[]{:S(2)}) collective-permute-start(s32[1,6]{1,0:T(1,128)S(1)} %get-tuple-element.15), channel_id=1, source_target_pairs={{0,20},{4,24},{8,28},{12,0},{16,4},{20,8},{24,12},{28,16},{1,21},{... | collective-permute-start | bytes 80 | tf_op jit(solution)/shard_map/ppermute | solution.py:16
  17.4 16.3 %all-to-all-start = ((bf16[8,2,128]{2,1,0:T(2,128)(2,1)}), bf16[8,2,128]{2,1,0:T(2,128)(2,1)S(1)}, u32[]{:S(2)}, u32[]{:S(2)}) async-start(bf16[8,2,128]{2,1,0:T(2,128)(2,1)} %reshape.287), calls=%async_computation | async-start | bytes 8192 | tf_op jit(solution)/shard_map/all_to_all | solution.py:54
  21.5 5.3 %collective-permute-start.1 = (s32[1,6]{1,0:T(1,128)S(1)}, s32[1,6]{1,0:T(1,128)S(1)}, u32[]{:S(2)}, u32[]{:S(2)}) collective-permute-start(s32[1,6]{1,0:T(1,128)S(1)} %get-tuple-element.16), channel_id=1, source_target_pairs={{0,24},{4,28},{8,0},{12,4},{16,8},{20,12},{24,16},{28,20},{1,25},{... | collective-permute-start | bytes 80 | tf_op jit(solution)/shard_map/ppermute | solution.py:16
  25.2 3.6 %collective-permute-start = (s32[1,6]{1,0:T(1,128)S(1)}, s32[1,6]{1,0:T(1,128)S(1)}, u32[]{:S(2)}, u32[]{:S(2)}) collective-permute-start(s32[1,6]{1,0:T(1,128)S(1)} %get-tuple-element.17), channel_id=1, source_target_pairs={{0,28},{4,0},{8,4},{12,8},{16,12},{20,16},{24,20},{28,24},{1,29},{... | collective-permute-start | bytes 80 | tf_op jit(solution)/shard_map/ppermute | solution.py:16
  33.7 13.8 %all-to-all-start.1 = ((bf16[8,6,2048]{2,1,0:T(8,128)(2,1)}), bf16[8,6,2048]{2,1,0:T(8,128)(2,1)}, u32[]{:S(2)}, u32[]{:S(2)}) async-start(bf16[8,6,2048]{2,1,0:T(8,128)(2,1)} %broadcast_select_fusion), calls=%async_computation.1 | async-start | bytes 524288 | tf_op jit(solution)/shard_map/all_to_all | solution.py:58
  55.7 11.6 %all-to-all-start.2 = ((bf16[8,6,2048]{2,1,0:T(8,128)(2,1)}), bf16[8,6,2048]{2,1,0:T(8,128)(2,1)S(1)}, u32[]{:S(2)}, u32[]{:S(2)}) async-start(bf16[8,6,2048]{2,1,0:T(8,128)(2,1)} %reshape.239), calls=%async_computation.2 | async-start | bytes 524288 | tf_op jit(solution)/shard_map/all_to_all | solution.py:62
